TPU v7x, 32 devices: a whole 2x2x4 slice. The times are simulated.
32 devices in a mesh: blk: 8 (over z, x), dp: 4 (over y, core).
Axes of the slice: x: 2, y: 2, z: 4, core: 2. Of those that a mesh axis runs over, the one named last changes fastest.
Arguments:
- tokens: bfloat16 [4096, 3072], P(('blk', 'dp')), may hold values from -6 to 6
- expert_ids: int32 [4096, 2], P(('blk', 'dp')), may hold values from 0 to 7, as said below
- gate_num: int32 [4096], P(('blk', 'dp')), may hold values from 1 to 255
- gate_weight: bfloat16 [3072, 8192], P('dp', 'blk'), may hold values from -0.109375 to 0.109375
- up_weight: bfloat16 [3072, 8192], P('dp', 'blk'), may hold values from -0.109375 to 0.109375
- down_weight: bfloat16 [8192, 3072], P(('blk', 'dp')), may hold values from -0.0625 to 0.0625
Outputs:
- moe_out: bfloat16 [4096, 3072], P(('blk', 'dp'))
Inputs may be any that keep to these rules, and one draw needn't show every extreme that they name: `expert_ids`: each row names two different experts. Among the 128 rows of one device (aligned blocks), between 1 and 64 name expert 0, and in every draw the rows of some device include exactly 64 such rows.
All inputs are finite; a program needn't handle non-finite values.
Results may differ from a plain program's by a relative error of at most 0.018.
Values may be sent and summed in bfloat16 or wider, within the bound.
A program may use at most 192 MiB of HBM per device.

v0:
```python
import jax
import jax.numpy as jnp
from jax import lax
from jax.sharding import PartitionSpec as P

GATE_SCALE = 256.0


def route_table(expert_ids, slot_count):
    hits = jnp.sum((expert_ids == 0).astype(jnp.int32), axis=1)
    position = jnp.cumsum(hits) - 1
    marks = (hits[:, None] > 0) & (
        position[:, None] == jnp.arange(slot_count, dtype=jnp.int32)[None, :]
    )
    return marks.astype(jnp.float32)


def gate_values(expert_ids, gate_num):
    first = gate_num.astype(jnp.float32) / GATE_SCALE
    return jnp.where(expert_ids[:, 0] == 0, first, 0.0) + jnp.where(
        expert_ids[:, 1] == 0, 1.0 - first, 0.0
    )


def on_device(tokens, expert_ids, gate_num, gate_weight, up_weight, down_weight):
    slot_count = tokens.shape[0] // 2
    marks = route_table(expert_ids, slot_count)
    packed = lax.dot_general(
        marks.astype(jnp.bfloat16),
        tokens,
        (((0,), (0,)), ((), ())),
        preferred_element_type=jnp.float32,
    ).astype(jnp.bfloat16)
    down_local = lax.all_gather(down_weight, "dp", axis=0, tiled=True)
    gathered = lax.all_gather(packed, "blk", axis=0, tiled=True)

    def add_rows(piece):
        return jnp.dot(gathered, piece, preferred_element_type=jnp.float32)

    gate = add_rows(lax.all_gather(gate_weight, "dp", axis=0, tiled=True))
    up = add_rows(lax.all_gather(up_weight, "dp", axis=0, tiled=True))
    hidden = (jax.nn.silu(gate) * up).astype(jnp.bfloat16)
    term = jnp.dot(hidden, down_local, preferred_element_type=jnp.float32).astype(jnp.bfloat16)
    term = lax.optimization_barrier(term)
    own_rows = lax.psum_scatter(
        term.astype(jnp.float32).astype(jnp.bfloat16), "blk", scatter_dimension=0, tiled=True
    ).astype(jnp.float32)
    expanded = jnp.dot(marks, own_rows, precision=lax.Precision.HIGHEST)
    weights = gate_values(expert_ids, gate_num)
    return (weights[:, None] * expanded).astype(jnp.bfloat16)


def solution(mesh):
    return jax.shard_map(
        on_device,
        mesh=mesh,
        in_specs=(
            P(("blk", "dp"), None),
            P(("blk", "dp"), None),
            P(("blk", "dp")),
            P("dp", "blk"),
            P("dp", "blk"),
            P(("blk", "dp"), None),
        ),
        out_specs=P(("blk", "dp"), None),
        check_vma=False,
    )
```

profile of v0, /device:TPU:0, one launch (start us, length us, event | category | flops | bytes accessed | tf_op | source)
XLA Modules:
  0.0 311.9 jit_solution(8863363476095033535)
XLA Ops:
  6.5 0.0 copy-start
  6.5 0.0 all-gather.5.cloned.1.call-start
  6.5 0.8 fusion.7
  7.3 0.1 copy.8
  7.4 0.2 reduce-window.8
  7.6 0.1 add_reduce_fusion
  7.7 0.0 copy-done
  7.7 1.1 convolution_convert_fusion.1
  8.9 0.0 all-gather.5.cloned.1.call-update
  8.9 0.0 all-gather.7.cloned.1.call-start
  8.9 0.7 all-gather.7.cloned.1.call-update
  9.6 0.0 all-gather.11.cloned.1.call-start
  9.7 0.7 all-gather.11.cloned.1.call-update
  10.4 0.0 all-gather.9.cloned.1.call-start
  10.4 0.5 all-gather.9.cloned.1.call-update
  10.9 0.0 reduce-scatter.2.cloned.1.call-start
  11.0 61.3 %all-gather.5.cloned.1.call-done = bf16[512,3072]{1,0:T(8,128)(2,1)} async-done(((bf16[64,3072]{1,0:T(8,128)(2,1)}), bf16[512,3072]{1,0:T(8,128)(2,1)}) %all-gather.5.cloned.1.call-update) | async-done | bytes 3145744 | tf_op jit(solution)/shard_map/all_gather | solution.py:35
  72.3 46.6 %all-gather.7.cloned.1.call-done = bf16[3072,1024]{1,0:T(8,128)(2,1)} async-done(((bf16[768,1024]{1,0:T(8,128)(2,1)}), bf16[3072,1024]{1,0:T(8,128)(2,1)}) %all-gather.7.cloned.1.call-update) | async-done | bytes 6291472 | tf_op jit(solution)/shard_map/all_gather | solution.py:40
  118.9 6.4 %fusion.10 = f32[512,1024]{1,0:T(8,128)S(1)} fusion(bf16[512,3072]{1,0:T(8,128)(2,1)} %all-gather.5.cloned.1.call-done, bf16[3072,1024]{1,0:T(8,128)(2,1)} %all-gather.7.cloned.1.call-done), kind=kOutput, calls=%fused_computation.20 | convolution fusion | flops 3221225472 | bytes 11534336 | tf_op jit(solution)/shard_map/dot_general | solution.py:38
  125.4 41.5 %all-gather.11.cloned.1.call-done = bf16[1024,3072]{1,0:T(8,128)(2,1)} async-done(((bf16[256,3072]{1,0:T(8,128)(2,1)}), bf16[1024,3072]{1,0:T(8,128)(2,1)}) %all-gather.11.cloned.1.call-update) | async-done | bytes 6291472 | tf_op jit(solution)/shard_map/all_gather | solution.py:34
  166.9 47.8 %all-gather.9.cloned.1.call-done = bf16[3072,1024]{1,0:T(8,128)(2,1)} async-done(((bf16[768,1024]{1,0:T(8,128)(2,1)}), bf16[3072,1024]{1,0:T(8,128)(2,1)}) %all-gather.9.cloned.1.call-update) | async-done | bytes 6291472 | tf_op jit(solution)/shard_map/all_gather | solution.py:41
  214.7 14.0 %convolution_convert_fusion = bf16[512,3072]{1,0:T(8,128)(2,1)} fusion(bf16[1024,3072]{1,0:T(8,128)(2,1)} %all-gather.11.cloned.1.call-done, f32[512,1024]{1,0:T(8,128)S(1)} %fusion.10, bf16[512,3072]{1,0:T(8,128)(2,1)} %all-gather.5.cloned.1.call-done, bf16[3072,1024]{1,0:T(8,128)(2,1)} %all-gather.9.cloned.1.call-done), kind=kOutput, calls=%fused_computation | convolution fusion | flops 6447169536 | bytes 20971520 | tf_op jit(solution)/shard_map/dot_general | solution.py:43
  228.6 0.0 copy-start.1
  228.6 0.0 copy-start.2
  228.6 0.0 reduce-scatter.2.cloned.1.call-update
  228.7 0.7 copy-done.1
  229.3 0.0 copy-done.2
  229.3 73.7 %reduce-scatter.2.cloned.1.call-done = bf16[64,3072]{1,0:T(8,128)(2,1)} async-done(((bf16[512,3072]{1,0:T(8,128)(2,1)}), bf16[64,3072]{1,0:T(8,128)(2,1)}) %reduce-scatter.2.cloned.1.call-update) | async-done | bytes 393232 | tf_op jit(solution)/shard_map/reduce_scatter | solution.py:45
  303.1 2.3 fusion
  (2 shorter events, 0.0 us)
Async XLA Ops:
  6.5 1.2 copy-start
  6.5 65.7 %all-gather.5.cloned.1.call-start = ((), (), s32[]{:S(2)}) async-start(), calls=%async_computation.1 | async-start | bytes 3538944 | tf_op jit(solution)/shard_map/all_gather | solution.py:35
  8.9 110.0 %all-gather.7.cloned.1.call-start = ((), (), s32[]{:S(2)}) async-start(), calls=%async_computation.2 | async-start | bytes 7864320 | tf_op jit(solution)/shard_map/all_gather | solution.py:40
  9.6 157.2 %all-gather.11.cloned.1.call-start = ((), (), s32[]{:S(2)}) async-start(), calls=%async_computation.4 | async-start | bytes 7864320 | tf_op jit(solution)/shard_map/all_gather | solution.py:34
  10.4 204.3 %all-gather.9.cloned.1.call-start = ((), (), s32[]{:S(2)}) async-start(), calls=%async_computation.3 | async-start | bytes 7864320 | tf_op jit(solution)/shard_map/all_gather | solution.py:41
  10.9 292.1 %reduce-scatter.2.cloned.1.call-start = ((), (), s32[]{:S(2)}) async-start(), calls=%async_computation.5 | async-start | bytes 3538944 | tf_op jit(solution)/shard_map/reduce_scatter | solution.py:45
  228.6 0.7 copy-start.1
  228.6 0.7 copy-start.2
Sparse Core Ops, SparseCore 0:
  9.5 62.7 all-gather.4
  73.8 45.0 all-gather.6
  120.5 46.3 all-gather.10
  168.3 46.3 all-gather.8
  228.8 74.2 reduce-scatter.1
where the time goes:
time: 312 us
  waiting for transfers between devices  273 us (88%)
  matrix products  23.8 us (8%)
  between operations  13.2 us (4%)
    reduce_scatter x1, waiting for transfers between devices, on_device(): lax.psum_scatter(term.astype(jnp.float32).astype(jnp.bfloat16), 'blk', sc...  73.7 us
    all_gather x1, waiting for transfers between devices, on_device(): gathered = lax.all_gather(packed, 'blk', axis=0, tiled=True)  61.3 us
    all_gather x1, waiting for transfers between devices, on_device(): up = add_rows(lax.all_gather(up_weight, 'dp', axis=0, tiled=True))  47.8 us
    all_gather x1, waiting for transfers between devices, on_device(): gate = add_rows(lax.all_gather(gate_weight, 'dp', axis=0, tiled=True))  46.6 us
    all_gather x1, waiting for transfers between devices, on_device(): down_local = lax.all_gather(down_weight, 'dp', axis=0, tiled=True)  41.5 us
    dot_general x1, matrix products, on_device(): jnp.dot(hidden, down_local, preferred_element_type=jnp.float32)  14 us
    dot_general x1, matrix products, add_rows(): return jnp.dot(gathered, piece, preferred_element_type=jnp.float32)  6.44 us
  transfers between devices with their start and end apart: 5, of which 5 were waited for; matrix products, arithmetic and copies ran while one was open for 2% of the time, Pallas kernels for 0%

commit v1 on v0

--- a/solution.py
+++ b/solution.py
@@ -2,6 +2,7 @@
 import jax.numpy as jnp
 from jax import lax
 from jax.sharding import PartitionSpec as P
+from jax.lax import axis_index, axis_size, ppermute
 
 GATE_SCALE = 256.0
 
@@ -31,7 +32,17 @@
         (((0,), (0,)), ((), ())),
         preferred_element_type=jnp.float32,
     ).astype(jnp.bfloat16)
-    down_local = lax.all_gather(down_weight, "dp", axis=0, tiled=True)
+    n_all = axis_size("dp")
+    e_now = [(k0 - 1, k0) for k0 in range(1, n_all)] + [(n_all - 1, 0)]
+    seen_now = down_weight
+    rack = [seen_now]
+    c = 0
+    while c < n_all - 1:
+        seen_now = ppermute(seen_now, axis_name="dp", perm=e_now)
+        rack += [seen_now]
+        c += 1
+    outer = jnp.concatenate([*reversed(rack)], axis=0)
+    down_local = jnp.roll(outer, (axis_index("dp") + 1) * seen_now.shape[0], axis=0)
     gathered = lax.all_gather(packed, "blk", axis=0, tiled=True)
 
     def add_rows(piece):

time: 312 us -> 265 us (0.85)
  waiting for transfers between devices: 273 us -> 205 us
  local copies, waits for them, and re-layouts: 0.77 us -> 18.1 us
    all_gather x1, waiting for transfers between devices: 61.3 us -> 0.01 us  [on_device(): gathered = lax.all_gather(packed, 'blk', axis=0, tiled=True)]
    ppermute x0 -> x3, waiting for transfers between devices: none -> 60.1 us  [on_device(): seen_now = ppermute(seen_now, axis_name='dp', perm=e_now)]
    all_gather x1 -> x0, waiting for transfers between devices: 41.5 us -> none  [on_device(): down_local = lax.all_gather(down_weight, 'dp', axis=0, tiled=True)]
    all_gather x1, waiting for transfers between devices: 46.6 us -> 30.4 us  [on_device(): gate = add_rows(lax.all_gather(gate_weight, 'dp', axis=0, tiled=True))]
    unnamed x6 -> x19, local copies, waits for them, and re-layouts: 0.66 us -> 16.7 us
    all_gather x1, waiting for transfers between devices: 47.8 us -> 39.4 us  [on_device(): up = add_rows(lax.all_gather(up_weight, 'dp', axis=0, tiled=True))]
  transfers between devices with their start and end apart: 5 -> 7, of which waited for: 5 -> 6; matrix products, arithmetic and copies ran while one was open for 2% -> 9% of each run, Pallas kernels for 0% -> 0%
where the time goes in v1:
time: 265 us
  waiting for transfers between devices  205 us (77%)
  matrix products  26.5 us (10%)
  local copies, waits for them, and re-layouts  18.1 us (7%)
  between operations  13.2 us (5%)
    reduce_scatter x1, waiting for transfers between devices, on_device(): lax.psum_scatter(term.astype(jnp.float32).astype(jnp.bfloat16), 'blk', sc...  73.9 us
    ppermute x3, waiting for transfers between devices, on_device(): seen_now = ppermute(seen_now, axis_name='dp', perm=e_now)  60.1 us
    all_gather x1, waiting for transfers between devices, on_device(): up = add_rows(lax.all_gather(up_weight, 'dp', axis=0, tiled=True))  39.4 us
    all_gather x1, waiting for transfers between devices, on_device(): gate = add_rows(lax.all_gather(gate_weight, 'dp', axis=0, tiled=True))  30.4 us
    unnamed x19, local copies, waits for them, and re-layouts  16.7 us
    dot_general x1, matrix products, on_device(): jnp.dot(hidden, down_local, preferred_element_type=jnp.float32)  14.5 us
    dot_general x1, matrix products, add_rows(): return jnp.dot(gathered, piece, preferred_element_type=jnp.float32)  8.58 us
  transfers between devices with their start and end apart: 7, of which 6 were waited for; matrix products, arithmetic and copies ran while one was open for 9% of the time, Pallas kernels for 0%

profile of v1, /device:TPU:0, one launch (start us, length us, event | category | flops | bytes accessed | tf_op | source)
XLA Modules:
  0.0 264.7 jit_solution(4907145526455168116)
XLA Ops:
  6.5 0.8 fusion.12
  7.4 0.1 copy.8
  7.5 0.2 reduce-window.8
  7.7 0.1 add_reduce_fusion
  7.8 1.1 convolution_convert_fusion
  8.9 0.0 all-gather.4.cloned.1.call-update
  9.0 0.0 all-gather.6.cloned.1.call-start
  9.0 0.7 all-gather.6.cloned.1.call-update
  9.7 0.0 all-gather.8.cloned.1.call-start
  9.8 0.7 all-gather.8.cloned.1.call-update
  10.4 0.0 reduce-scatter.2.cloned.1.call-start
  10.5 0.5 collective-permute-start
  11.0 20.0 %collective-permute-done = bf16[256,3072]{1,0:T(8,128)(2,1)S(1)} collective-permute-done((bf16[256,3072]{1,0:T(8,128)(2,1)S(1)}, bf16[256,3072]{1,0:T(8,128)(2,1)S(1)}, u32[]{:S(2)}, u32[]{:S(2)}) %collective-permute-start) | collective-permute-done | bytes 1572896 | tf_op jit(solution)/shard_map/ppermute | solution.py:41
  31.1 1.2 copy-done.2
  32.3 19.9 %collective-permute-done.1 = bf16[256,3072]{1,0:T(8,128)(2,1)} collective-permute-done((bf16[256,3072]{1,0:T(8,128)(2,1)S(1)}, bf16[256,3072]{1,0:T(8,128)(2,1)}, u32[]{:S(2)}, u32[]{:S(2)}) %collective-permute-start.1) | collective-permute-done | bytes 1572896 | tf_op jit(solution)/shard_map/ppermute | solution.py:41
  52.2 20.2 %collective-permute-done.2 = bf16[256,3072]{1,0:T(8,128)(2,1)} collective-permute-done((bf16[256,3072]{1,0:T(8,128)(2,1)}, bf16[256,3072]{1,0:T(8,128)(2,1)}, u32[]{:S(2)}, u32[]{:S(2)}) %collective-permute-start.2) | collective-permute-done | bytes 1572896 | tf_op jit(solution)/shard_map/ppermute | solution.py:41
  72.4 2.7 %constant_dynamic-update-slice_fusion.7 = bf16[2048,3072]{1,0:T(8,128)(2,1)} fusion(bf16[256,3072]{1,0:T(8,128)(2,1)} %collective-permute-done.2), kind=kLoop, calls=%fused_computation.22 | loop fusion | bytes 3145728
  75.0 2.7 %constant_dynamic-update-slice_fusion.6 = bf16[2048,3072]{1,0:T(8,128)(2,1)} fusion(bf16[2048,3072]{1,0:T(8,128)(2,1)} %constant_dynamic-update-slice_fusion.7, bf16[256,3072]{1,0:T(8,128)(2,1)} %collective-permute-done.1), kind=kLoop, calls=%fused_computation.21 | loop fusion | bytes 3145728
  77.7 1.3 constant_dynamic-update-slice_fusion.5
  78.9 1.3 constant_dynamic-update-slice_fusion.4
  80.2 2.9 %constant_dynamic-update-slice_fusion.3 = bf16[2048,3072]{1,0:T(8,128)(2,1)} fusion(bf16[2048,3072]{1,0:T(8,128)(2,1)} %constant_dynamic-update-slice_fusion.4, bf16[256,3072]{1,0:T(8,128)(2,1)} %collective-permute-done.2), kind=kLoop, calls=%fused_computation.18 | loop fusion | bytes 3145728
  83.1 2.9 %constant_dynamic-update-slice_fusion.2 = bf16[2048,3072]{1,0:T(8,128)(2,1)} fusion(bf16[2048,3072]{1,0:T(8,128)(2,1)} %constant_dynamic-update-slice_fusion.3, bf16[256,3072]{1,0:T(8,128)(2,1)} %collective-permute-done.1), kind=kLoop, calls=%fused_computation.17 | loop fusion | bytes 3145728
  86.0 1.3 constant_dynamic-update-slice_fusion.1
  87.2 1.3 constant_dynamic-update-slice_fusion
  88.5 30.4 %all-gather.6.cloned.1.call-done = bf16[3072,1024]{1,0:T(8,128)(2,1)} async-done(((bf16[768,1024]{1,0:T(8,128)(2,1)}), bf16[3072,1024]{1,0:T(8,128)(2,1)}) %all-gather.6.cloned.1.call-update) | async-done | bytes 6291472 | tf_op jit(solution)/shard_map/all_gather | solution.py:51
  118.9 8.6 %fusion.16 = f32[512,1024]{1,0:T(8,128)} fusion(bf16[512,3072]{1,0:T(8,128)(2,1)} %all-gather.4.cloned.1.call-done, bf16[3072,1024]{1,0:T(8,128)(2,1)} %all-gather.6.cloned.1.call-done), kind=kOutput, calls=%fused_computation.31 | convolution fusion | flops 3221225472 | bytes 11534336 | tf_op jit(solution)/shard_map/dot_general | solution.py:49
  127.5 39.4 %all-gather.8.cloned.1.call-done = bf16[3072,1024]{1,0:T(8,128)(2,1)} async-done(((bf16[768,1024]{1,0:T(8,128)(2,1)}), bf16[3072,1024]{1,0:T(8,128)(2,1)}) %all-gather.8.cloned.1.call-update) | async-done | bytes 6291472 | tf_op jit(solution)/shard_map/all_gather | solution.py:52
  166.9 14.5 %fusion.2 = bf16[512,3072]{1,0:T(8,128)(2,1)} fusion(bf16[2048,3072]{1,0:T(8,128)(2,1)} %constant_dynamic-update-slice_fusion, s32[]{:T(128)S(6)} %select_n.23, f32[512,1024]{1,0:T(8,128)} %fusion.16, bf16[512,3072]{1,0:T(8,128)(2,1)} %all-gather.4.cloned.1.call-done, bf16[3072,1024]{1,0:T(8,128)(2,1)} %all-gather.8.cloned.1.call-done), kind=kOutput, calls=%fused_computation.2 | convolution fusion | flops 6447169536 | bytes 20971524 | tf_op jit(solution)/shard_map/dot_general | solution.py:54
  181.4 0.0 reduce-scatter.2.cloned.1.call-update
  181.4 0.7 copy-done.4
  182.0 73.9 %reduce-scatter.2.cloned.1.call-done = bf16[64,3072]{1,0:T(8,128)(2,1)} async-done(((bf16[512,3072]{1,0:T(8,128)(2,1)}), bf16[64,3072]{1,0:T(8,128)(2,1)}) %reduce-scatter.2.cloned.1.call-update) | async-done | bytes 393232 | tf_op jit(solution)/shard_map/reduce_scatter | solution.py:56
  255.9 2.3 fusion.5
  (16 shorter events, 0.0 us)
Async XLA Ops:
  6.5 1.3 copy-start
  6.5 4.0 %copy-start.1 = (bf16[256,3072]{1,0:T(8,128)(2,1)S(1)}, bf16[256,3072]{1,0:T(8,128)(2,1)}, u32[]{:S(2)}) copy-start(bf16[256,3072]{1,0:T(8,128)(2,1)} %param.11) | copy-start | bytes 4718596
  6.5 81.9 %all-gather.4.cloned.1.call-start = ((), (), s32[]{:S(2)}) async-start(), calls=%async_computation.1 | async-start | bytes 3538944 | tf_op jit(solution)/shard_map/all_gather | solution.py:46
  9.0 109.9 %all-gather.6.cloned.1.call-start = ((), (), s32[]{:S(2)}) async-start(), calls=%async_computation.2 | async-start | bytes 7864320 | tf_op jit(solution)/shard_map/all_gather | solution.py:51
  9.7 157.2 %all-gather.8.cloned.1.call-start = ((), (), s32[]{:S(2)}) async-start(), calls=%async_computation.3 | async-start | bytes 7864320 | tf_op jit(solution)/shard_map/all_gather | solution.py:52
  10.4 245.5 %reduce-scatter.2.cloned.1.call-start = ((), (), s32[]{:S(2)}) async-start(), calls=%async_computation.4 | async-start | bytes 3538944 | tf_op jit(solution)/shard_map/reduce_scatter | solution.py:56
  10.5 20.6 %collective-permute-start = (bf16[256,3072]{1,0:T(8,128)(2,1)S(1)}, bf16[256,3072]{1,0:T(8,128)(2,1)S(1)}, u32[]{:S(2)}, u32[]{:S(2)}) collective-permute-start(bf16[256,3072]{1,0:T(8,128)(2,1)S(1)} %copy-done.1), channel_id=1, source_target_pairs={{0,1},{1,2},{2,3},{3,0},{4,5},{5,6},{6,7},{7,4},{8,9},{9,10},{10,1... | collective-permute-start | bytes 4718600 | tf_op jit(solution)/shard_map/ppermute | solution.py:41
  31.1 1.2 copy-start.2
  32.3 19.9 %collective-permute-start.1 = (bf16[256,3072]{1,0:T(8,128)(2,1)S(1)}, bf16[256,3072]{1,0:T(8,128)(2,1)}, u32[]{:S(2)}, u32[]{:S(2)}) collective-permute-start(bf16[256,3072]{1,0:T(8,128)(2,1)S(1)} %collective-permute-done), channel_id=1, source_target_pairs={{0,1},{1,2},{2,3},{3,0},{4,5},{5,6},{6,7},{7,4},{8,9},{9,10},{10,1... | collective-permute-start | bytes 4718600 | tf_op jit(solution)/shard_map/ppermute | solution.py:41
  52.2 20.2 %collective-permute-start.2 = (bf16[256,3072]{1,0:T(8,128)(2,1)}, bf16[256,3072]{1,0:T(8,128)(2,1)}, u32[]{:S(2)}, u32[]{:S(2)}) collective-permute-start(bf16[256,3072]{1,0:T(8,128)(2,1)} %collective-permute-done.1), channel_id=1, source_target_pairs={{0,1},{1,2},{2,3},{3,0},{4,5},{5,6},{6,7},{7,4},{8,9},{9,10},{10,1... | collective-permute-start | bytes 4718600 | tf_op jit(solution)/shard_map/ppermute | solution.py:41
  52.2 25.5 %copy-start.3 = (bf16[256,3072]{1,0:T(8,128)(2,1)S(1)}, bf16[256,3072]{1,0:T(8,128)(2,1)}, u32[]{:S(2)}) copy-start(bf16[256,3072]{1,0:T(8,128)(2,1)} %copy-done.2) | copy-start | bytes 4718596
  181.4 0.7 copy-start.4
  181.4 0.7 copy-start.5
Sparse Core Ops, SparseCore 0:
  9.5 62.7 all-gather.3
  73.8 45.0 all-gather.5
  120.5 46.3 all-gather.7
  181.5 74.3 reduce-scatter.1
